TPU v7x, 32 devices: a whole 2x2x4 slice. The times are simulated.
32 devices in a mesh: ep: 4 (over z), fsdp: 8 (over y, x, core).
Axes of the slice: x: 2, y: 2, z: 4, core: 2. Of those that a mesh axis runs over, the one named last changes fastest.
Arguments:
- train_gate: float32 [64, 2048, 1408], P('ep', 'fsdp'), may hold values from -0.1875 to 0.1875
- train_up: float32 [64, 2048, 1408], P('ep', 'fsdp'), may hold values from -0.1875 to 0.1875
- train_down: float32 [64, 1408, 2048], P('ep', None, 'fsdp'), may hold values from -0.21875 to 0.21875
- router_weight: float32 [2048, 64], P('fsdp', 'ep'), may hold values from -0.125 to 0.125
- router_gain: float32 [2048], P('fsdp'), may hold values from 0.25 to 1.75
Outputs:
- ready_gate: bfloat16 [64, 2048, 1408], P('ep', None, 'fsdp')
- ready_up: bfloat16 [64, 2048, 1408], P('ep', None, 'fsdp')
- ready_down: bfloat16 [64, 1408, 2048], P('ep', 'fsdp')
- scale_gate: float32 [64, 1408], P('ep', 'fsdp')
- scale_up: float32 [64, 1408], P('ep', 'fsdp')
- scale_down: float32 [64, 1408], P('ep', 'fsdp')
- serve_router: bfloat16 [2048, 64], replicated
All inputs are finite; a program needn't handle non-finite values.
Results may differ from a plain program's by a relative error of at most 0.001.
Values may be sent and summed in bfloat16 or wider, within the bound.
A program may use at most 192 MiB of HBM per device.

v0:
```python
import jax
import jax.numpy as jnp
from jax import lax
from jax.sharding import PartitionSpec as P


def body(train_gate, train_up, train_down, router_weight, router_gain):
    total_gate, total_up, total_down = lax.psum(
        (
            jnp.sum(train_gate * train_gate, axis=1),
            jnp.sum(train_up * train_up, axis=1),
            jnp.sum(train_down * train_down, axis=2),
        ),
        "fsdp",
    )
    scale_gate = jnp.sqrt(total_gate)
    scale_up = jnp.sqrt(total_up)
    scale_down = jnp.sqrt(total_down)
    narrow_gate, narrow_up, narrow_down = (
        (train_gate / jnp.expand_dims(scale_gate, 1)).astype(jnp.bfloat16),
        (train_up / jnp.expand_dims(scale_up, 1)).astype(jnp.bfloat16),
        (train_down / jnp.expand_dims(scale_down, 2)).astype(jnp.bfloat16),
    )
    ready_gate, ready_up = (
        lax.all_to_all(narrow_gate, "fsdp", split_axis=2, concat_axis=1, tiled=True),
        lax.all_to_all(narrow_up, "fsdp", split_axis=2, concat_axis=1, tiled=True),
    )
    ready_down = lax.all_to_all(narrow_down, "fsdp", split_axis=1, concat_axis=2, tiled=True)
    scale_gate = lax.dynamic_slice_in_dim(
        scale_gate, lax.axis_index("fsdp") * ready_gate.shape[2], ready_gate.shape[2], axis=1
    )
    scale_up = lax.dynamic_slice_in_dim(
        scale_up, lax.axis_index("fsdp") * ready_up.shape[2], ready_up.shape[2], axis=1
    )
    scale_down = lax.dynamic_slice_in_dim(
        scale_down, lax.axis_index("fsdp") * ready_down.shape[1], ready_down.shape[1], axis=1
    )
    part_router = (router_weight * router_gain[:, None]).astype(jnp.bfloat16)
    row_router = lax.all_gather(part_router, "fsdp", axis=0, tiled=True)
    serve_router = lax.all_gather(row_router, "ep", axis=1, tiled=True)
    return (ready_gate, ready_up, ready_down, scale_gate, scale_up, scale_down, serve_router)


def solution(mesh):
    return jax.shard_map(
        body,
        mesh=mesh,
        in_specs=(
            P("ep", "fsdp", None),
            P("ep", "fsdp", None),
            P("ep", None, "fsdp"),
            P("fsdp", "ep"),
            P("fsdp"),
        ),
        out_specs=(
            P("ep", None, "fsdp"),
            P("ep", None, "fsdp"),
            P("ep", "fsdp", None),
            P("ep", "fsdp"),
            P("ep", "fsdp"),
            P("ep", "fsdp"),
            P(),
        ),
        check_vma=False,
    )
```

profile of v0, /device:TPU:0, one launch (start us, length us, event | category | flops | bytes accessed | tf_op | source)
XLA Modules:
  0.0 618.1 jit_solution(2208627624309375978)
XLA Ops:
  7.2 0.0 all-reduce.3.cloned.1.call-start
  7.2 9.2 %multiply_reduce_fusion = f32[16,1408]{1,0:T(8,128)} fusion(f32[16,1408,256]{2,1,0:T(8,128)} %param.7), kind=kLoop, calls=%fused_computation.2 | loop fusion | flops 11511808 | bytes 23158784 | tf_op jit(solution)/shard_map/reduce_sum | solution.py:12
  16.4 5.0 copy-done
  21.4 11.0 %multiply_reduce_fusion.1 = (f32[16,1408]{1,0:T(8,128)}, f32[16,1408]{1,0:T(8,128)}) fusion(f32[16,256,1408]{2,1,0:T(8,128)S(1)} %copy-done, f32[16,256,1408]{2,1,0:T(8,128)} %param.5), kind=kLoop, calls=%fused_computation.4 | loop fusion | flops 23023616 | bytes 46317568 | tf_op jit(solution)/shard_map/reduce_sum | solution.py:11
  32.5 0.0 all-reduce.3.cloned.1.call-update
  32.5 23.7 %copy.28 = f32[16,256,1408]{1,0,2:T(8,128)} copy(f32[16,256,1408]{2,1,0:T(8,128)} %param.6) | data formatting | bytes 46137344 | tf_op args[1]
  56.2 32.6 %all-reduce.3.cloned.1.call-done = (f32[16,1408]{1,0:T(8,128)}, f32[16,1408]{1,0:T(8,128)}, f32[16,1408]{1,0:T(8,128)}) async-done(((f32[16,1408]{1,0:T(8,128)}, f32[16,1408]{1,0:T(8,128)}, f32[16,1408]{1,0:T(8,128)}), (f32[16,1408]{1,0:T(8,128)}, f32[16,1408]{1,0:T(8,128)}, f32[16,1408]{1,0:T(8,128)})) %all-reduce.3.cloned.1.call-update) | async-done | bytes 270352 | tf_op jit(solution)/shard_map/psum | solution.py:8
  88.8 0.9 sqrt.10
  89.7 0.3 copy.27
  90.0 14.2 %divide_convert_fusion = bf16[16,256,1408]{1,0,2:T(8,128)(2,1)} fusion(f32[16,256,1408]{1,0,2:T(8,128)} %copy.28, f32[16,1408]{0,1:T(8,128)S(1)} %copy.27), kind=kLoop, calls=%fused_computation.3 | loop fusion | flops 11534336 | bytes 34693120 | tf_op jit(solution)/shard_map/convert_element_type | solution.py:21
  104.2 5.2 all-to-all-start.1
  109.5 23.7 %copy.24 = f32[16,256,1408]{1,0,2:T(8,128)} copy(f32[16,256,1408]{2,1,0:T(8,128)} %param.5) | data formatting | bytes 46137344 | tf_op args[0]
  133.2 0.3 copy.23
  133.5 14.2 %divide_convert_fusion.1 = bf16[16,256,1408]{1,0,2:T(8,128)(2,1)} fusion(f32[16,256,1408]{1,0,2:T(8,128)} %copy.24, f32[16,1408]{0,1:T(8,128)S(1)} %copy.23), kind=kLoop, calls=%fused_computation.5 | loop fusion | flops 11534336 | bytes 34693120 | tf_op jit(solution)/shard_map/convert_element_type | solution.py:20
  147.7 89.5 %all-to-all-done.1 = bf16[16,256,1408]{1,0,2:T(8,128)(2,1)} async-done(((bf16[16,256,1408]{1,0,2:T(8,128)(2,1)}), bf16[16,256,1408]{1,0,2:T(8,128)(2,1)}, u32[]{:S(2)}, u32[]{:S(2)}) %all-to-all-start.1) | async-done | bytes 11534368 | tf_op jit(solution)/shard_map/all_to_all | solution.py:26
  237.2 5.3 all-to-all-start
  242.5 0.3 copy.31
  242.8 32.6 %fusion = bf16[16,1408,256]{2,0,1:T(8,128)(2,1)} fusion(f32[16,1408,256]{2,1,0:T(8,128)} %param.7, f32[16,1408]{0,1:T(8,128)S(1)} %copy.31), kind=kLoop, calls=%fused_computation.1 | loop fusion | flops 11534336 | bytes 34693120 | tf_op jit(solution)/shard_map/convert_element_type | solution.py:22
  275.4 94.8 %all-to-all-done = bf16[16,256,1408]{1,0,2:T(8,128)(2,1)} async-done(((bf16[16,256,1408]{1,0,2:T(8,128)(2,1)}), bf16[16,256,1408]{1,0,2:T(8,128)(2,1)}, u32[]{:S(2)}, u32[]{:S(2)}) %all-to-all-start) | async-done | bytes 11534368 | tf_op jit(solution)/shard_map/all_to_all | solution.py:25
  370.2 5.3 all-to-all-start.2
  375.5 130.9 %all_gather.6 = bf16[2048,16]{0,1:T(8,128)(2,1)S(1)} all-gather(bf16[256,16]{0,1:T(8,128)(2,1)S(1)} %multiply_convert_fusion), channel_id=1, replica_groups=mesh['ep'=4,'fsdp'=8] {'fsdp'}, dimensions={0}, use_global_device_ids=true | all-gather | bytes 73728 | tf_op jit(solution)/shard_map/all_gather | solution.py:39
  506.4 14.2 %all_gather.7 = bf16[2048,64]{0,1:T(8,128)(2,1)S(1)} all-gather(bf16[2048,16]{0,1:T(8,128)(2,1)S(1)} %all_gather.6), channel_id=1, replica_groups=mesh['ep'=4,'fsdp'=8] {'ep'}, dimensions={1}, use_global_device_ids=true | all-gather | bytes 327680 | tf_op jit(solution)/shard_map/all_gather | solution.py:40
  520.6 0.7 constant_dynamic-slice_fusion
  521.3 0.7 constant_dynamic-slice_fusion.1
  522.0 0.7 constant_dynamic-slice_fusion.2
  522.6 11.3 %copy.30 = bf16[16,8,256,176]{2,1,3,0:T(8,128)(2,1)} copy(bf16[16,8,256,176]{2,0,3,1:T(8,128)(2,1)} %bitcast.5) | data formatting | bytes 23068672 | tf_op jit(solution)/shard_map/all_to_all | solution.py:26
  534.0 18.0 %all_to_all.46 = bf16[16,2048,176]{1,2,0:T(8,128)(2,1)} reshape(bf16[16,8,256,176]{2,1,3,0:T(8,128)(2,1)} %copy.30) | data formatting | bytes 23068672 | tf_op jit(solution)/shard_map/all_to_all | solution.py:26
  551.9 11.3 %copy.26 = bf16[16,8,256,176]{2,1,3,0:T(8,128)(2,1)} copy(bf16[16,8,256,176]{2,0,3,1:T(8,128)(2,1)} %bitcast.2) | data formatting | bytes 23068672 | tf_op jit(solution)/shard_map/all_to_all | solution.py:25
  563.3 18.0 %all_to_all.42 = bf16[16,2048,176]{1,2,0:T(8,128)(2,1)} reshape(bf16[16,8,256,176]{2,1,3,0:T(8,128)(2,1)} %copy.26) | data formatting | bytes 23068672 | tf_op jit(solution)/shard_map/all_to_all | solution.py:25
  581.2 11.3 %copy.33 = bf16[16,176,8,256]{3,2,1,0:T(8,128)(2,1)} copy(bf16[16,176,8,256]{3,0,1,2:T(8,128)(2,1)} %bitcast.7) | data formatting | bytes 23068672 | tf_op jit(solution)/shard_map/all_to_all | solution.py:28
  592.5 18.0 %all_to_all.50 = bf16[16,176,2048]{2,1,0:T(8,128)(2,1)} reshape(bf16[16,176,8,256]{3,2,1,0:T(8,128)(2,1)} %copy.33) | data formatting | bytes 23068672 | tf_op jit(solution)/shard_map/all_to_all | solution.py:28
  610.5 0.7 copy.43
  (13 shorter events, 0.1 us)
Async XLA Ops:
  7.2 81.6 %all-reduce.3.cloned.1.call-start = ((), (), s32[]{:S(2)}) async-start(), calls=%async_computation.3 | async-start | bytes 540672 | tf_op jit(solution)/shard_map/psum | solution.py:8
  7.2 14.2 %copy-start = (f32[16,256,1408]{2,1,0:T(8,128)S(1)}, f32[16,256,1408]{2,1,0:T(8,128)}, u32[]{:S(2)}) copy-start(f32[16,256,1408]{2,1,0:T(8,128)} %param.6) | copy-start | bytes 69206016
  104.2 133.0 %all-to-all-start.1 = ((bf16[16,256,1408]{1,0,2:T(8,128)(2,1)}), bf16[16,256,1408]{1,0,2:T(8,128)(2,1)}, u32[]{:S(2)}, u32[]{:S(2)}) async-start(bf16[16,256,1408]{1,0,2:T(8,128)(2,1)} %divide_convert_fusion), calls=%async_computation.1 | async-start | bytes 23068672 | tf_op jit(solution)/shard_map/all_to_all | solution.py:26
  109.5 23.7 %copy-start.2 = (f32[16,1408]{1,0:T(8,128)S(1)}, f32[16,1408]{1,0:T(8,128)}, u32[]{:S(2)}) copy-start(f32[16,1408]{1,0:T(8,128)} %get-tuple-element.7) | copy-start | bytes 270340
  133.5 109.0 %copy-start.1 = (f32[16,1408]{1,0:T(8,128)S(1)}, f32[16,1408]{1,0:T(8,128)}, u32[]{:S(2)}) copy-start(f32[16,1408]{1,0:T(8,128)} %get-tuple-element.9) | copy-start | bytes 270340
  237.2 133.0 %all-to-all-start = ((bf16[16,256,1408]{1,0,2:T(8,128)(2,1)}), bf16[16,256,1408]{1,0,2:T(8,128)(2,1)}, u32[]{:S(2)}, u32[]{:S(2)}) async-start(bf16[16,256,1408]{1,0,2:T(8,128)(2,1)} %divide_convert_fusion.1), calls=%async_computation | async-start | bytes 23068672 | tf_op jit(solution)/shard_map/all_to_all | solution.py:25
  242.8 132.7 %copy-start.3 = (f32[256,16]{0,1:T(8,128)S(1)}, f32[256,16]{0,1:T(8,128)}, u32[]{:S(2)}) copy-start(f32[256,16]{0,1:T(8,128)} %param.8) | copy-start | bytes 49156
  242.8 132.7 %copy-start.4 = (f32[256]{0:T(256)S(1)}, f32[256]{0:T(256)}, u32[]{:S(2)}) copy-start(f32[256]{0:T(256)} %param.9) | copy-start | bytes 3076
  370.2 211.0 %all-to-all-start.2 = ((bf16[16,1408,256]{2,0,1:T(8,128)(2,1)}), bf16[16,1408,256]{2,0,1:T(8,128)(2,1)}, u32[]{:S(2)}, u32[]{:S(2)}) async-start(bf16[16,1408,256]{2,0,1:T(8,128)(2,1)} %fusion), calls=%async_computation.2 | async-start | bytes 23068672 | tf_op jit(solution)/shard_map/all_to_all | solution.py:28
Sparse Core Ops, SparseCore 0:
  32.6 56.1 all-reduce.2
where the time goes:
time: 621 us; the launch traced here: 618 us
  waiting for transfers between devices  217 us (35%)
  local copies, waits for them, and re-layouts  145 us (23%)
  blocking collectives  145 us (23%)
  other arithmetic  81.3 us (13%)
  starting transfers between devices  15.8 us (3%)
  between operations  14.2 us (2%)
    all_gather x1, blocking collectives, body(): row_router = lax.all_gather(part_router, 'fsdp', axis=0, tiled=True)  131 us
    all_to_all x1, waiting for transfers between devices, body(): lax.all_to_all(narrow_gate, 'fsdp', split_axis=2, concat_axis=1, tiled=True)  94.8 us
    all_to_all x1, waiting for transfers between devices, body(): lax.all_to_all(narrow_up, 'fsdp', split_axis=2, concat_axis=1, tiled=True)  89.5 us
    unnamed x13, local copies, waits for them, and re-layouts  53.2 us
    psum x1, waiting for transfers between devices, body(): lax.psum((jnp.sum(train_gate * train_gate, axis=1), jnp.sum(train_up * tr...  32.6 us
    convert_element_type x1, other arithmetic, body(): (train_down / jnp.expand_dims(scale_down, 2)).astype(jnp.bfloat16)  32.6 us
    all_to_all x2, local copies, waits for them, and re-layouts, body(): lax.all_to_all(narrow_up, 'fsdp', split_axis=2, concat_axis=1, tiled=True)  29.3 us
    all_to_all x2, local copies, waits for them, and re-layouts, body(): lax.all_to_all(narrow_gate, 'fsdp', split_axis=2, concat_axis=1, tiled=True)  29.3 us
  transfers between devices with their start and end apart: 4, of which 3 were waited for; matrix products, arithmetic and copies ran while one was open for 19% of the time, Pallas kernels for 0%

commit v1 on v0

--- a/solution.py
+++ b/solution.py
@@ -25,7 +25,12 @@
         lax.all_to_all(narrow_gate, "fsdp", split_axis=2, concat_axis=1, tiled=True),
         lax.all_to_all(narrow_up, "fsdp", split_axis=2, concat_axis=1, tiled=True),
     )
-    ready_down = lax.all_to_all(narrow_down, "fsdp", split_axis=1, concat_axis=2, tiled=True)
+    ready_down = jnp.concatenate(
+        lax.all_to_all(
+            jnp.stack(jnp.split(narrow_down, lax.axis_size("fsdp"), axis=1)), "fsdp", 0, 0
+        ),
+        axis=2,
+    )
     scale_gate = lax.dynamic_slice_in_dim(
         scale_gate, lax.axis_index("fsdp") * ready_gate.shape[2], ready_gate.shape[2], axis=1
     )

time: 621 us -> 601 us (0.968)
  other arithmetic: 81.3 us -> 58.4 us
  waiting for transfers between devices: 217 us -> 230 us
  local copies, waits for them, and re-layouts: 145 us -> 135 us
    all_to_all x2 -> x0, local copies, waits for them, and re-layouts: 29.3 us -> none  [body(): lax.all_to_all(narrow_down, 'fsdp', split_axis=1, concat_axis=2, tiled=True)]
    convert_element_type x1, other arithmetic: 32.6 us -> 9.8 us  [body(): (train_down / jnp.expand_dims(scale_down, 2)).astype(jnp.bfloat16)]
    all_to_all x1, waiting for transfers between devices: 89.5 us -> 108 us  [body(): lax.all_to_all(narrow_up, 'fsdp', split_axis=2, concat_axis=1, tiled=True)]
    reshape x0 -> x1, local copies, waits for them, and re-layouts: none -> 10 us  [body(): jnp.concatenate(lax.all_to_all(jnp.stack(jnp.split(narrow_down, lax.axis_...]
    unnamed x13 -> x20, local copies, waits for them, and re-layouts: 53.2 us -> 61.6 us
  transfers between devices with their start and end apart: 4 -> 4, of which waited for: 3 -> 3; matrix products, arithmetic and copies ran while one was open for 19% -> 18% of each run, Pallas kernels for 0% -> 0%
where the time goes in v1:
time: 601 us; the launch traced here: 599 us
  waiting for transfers between devices  230 us (38%)
  blocking collectives  145 us (24%)
  local copies, waits for them, and re-layouts  135 us (22%)
  other arithmetic  58.4 us (10%)
  starting transfers between devices  15.8 us (3%)
  between operations  14.2 us (2%)
    all_gather x1, blocking collectives, body(): row_router = lax.all_gather(part_router, 'fsdp', axis=0, tiled=True)  131 us
    all_to_all x1, waiting for transfers between devices, body(): lax.all_to_all(narrow_up, 'fsdp', split_axis=2, concat_axis=1, tiled=True)  108 us
    all_to_all x1, waiting for transfers between devices, body(): lax.all_to_all(narrow_gate, 'fsdp', split_axis=2, concat_axis=1, tiled=True)  89.5 us
    unnamed x20, local copies, waits for them, and re-layouts  61.6 us
    psum x1, waiting for transfers between devices, body(): lax.psum((jnp.sum(train_gate * train_gate, axis=1), jnp.sum(train_up * tr...  32.6 us
    all_to_all x2, local copies, waits for them, and re-layouts, body(): lax.all_to_all(narrow_gate, 'fsdp', split_axis=2, concat_axis=1, tiled=True)  29.3 us
    all_to_all x2, local copies, waits for them, and re-layouts, body(): lax.all_to_all(narrow_up, 'fsdp', split_axis=2, concat_axis=1, tiled=True)  29.3 us
    convert_element_type x1, other arithmetic, body(): (train_gate / jnp.expand_dims(scale_gate, 1)).astype(jnp.bfloat16)  14.2 us
  transfers between devices with their start and end apart: 4, of which 3 were waited for; matrix products, arithmetic and copies ran while one was open for 18% of the time, Pallas kernels for 0%

profile of v1, /device:TPU:0, one launch (start us, length us, event | category | flops | bytes accessed | tf_op | source)
XLA Modules:
  0.0 598.6 jit_solution(13294843355749085687)
XLA Ops:
  7.2 9.2 %multiply_reduce_fusion = f32[16,1408]{1,0:T(8,128)} fusion(f32[16,1408,256]{2,1,0:T(8,128)} %param.7), kind=kLoop, calls=%fused_computation.1 | loop fusion | flops 11511808 | bytes 23158784 | tf_op jit(solution)/shard_map/reduce_sum | solution.py:12
  16.4 5.0 copy-done
  21.4 11.0 %multiply_reduce_fusion.1 = (f32[16,1408]{1,0:T(8,128)}, f32[16,1408]{1,0:T(8,128)}) fusion(f32[16,256,1408]{2,1,0:T(8,128)} %param.6, f32[16,256,1408]{2,1,0:T(8,128)S(1)} %copy-done), kind=kLoop, calls=%fused_computation.3 | loop fusion | flops 23023616 | bytes 46317568 | tf_op jit(solution)/shard_map/reduce_sum | solution.py:11
  32.5 23.7 %copy.24 = f32[16,256,1408]{1,0,2:T(8,128)} copy(f32[16,256,1408]{2,1,0:T(8,128)} %param.5) | data formatting | bytes 46137344 | tf_op args[0]
  56.2 32.6 %all-reduce.3.cloned.1.call-done = (f32[16,1408]{1,0:T(8,128)}, f32[16,1408]{1,0:T(8,128)}, f32[16,1408]{1,0:T(8,128)}) async-done(((f32[16,1408]{1,0:T(8,128)}, f32[16,1408]{1,0:T(8,128)}, f32[16,1408]{1,0:T(8,128)}), (f32[16,1408]{1,0:T(8,128)}, f32[16,1408]{1,0:T(8,128)}, f32[16,1408]{1,0:T(8,128)})) %all-reduce.3.cloned.1.call-update) | async-done | bytes 270352 | tf_op jit(solution)/shard_map/psum | solution.py:8
  88.8 0.9 sqrt.9
  90.0 14.2 %divide_convert_fusion.2 = bf16[16,256,1408]{1,0,2:T(8,128)(2,1)} fusion(f32[16,256,1408]{1,0,2:T(8,128)} %copy.24, f32[16,1408]{0,1:T(8,128)S(1)} %copy.23), kind=kLoop, calls=%fused_computation.4 | loop fusion | flops 11534336 | bytes 34693120 | tf_op jit(solution)/shard_map/convert_element_type | solution.py:20
  104.2 5.2 all-to-all-start
  109.4 23.7 %copy.28 = f32[16,256,1408]{1,0,2:T(8,128)} copy(f32[16,256,1408]{2,1,0:T(8,128)} %param.6) | data formatting | bytes 46137344 | tf_op args[1]
  133.4 14.2 %divide_convert_fusion.1 = bf16[16,256,1408]{1,0,2:T(8,128)(2,1)} fusion(f32[16,256,1408]{1,0,2:T(8,128)} %copy.28, f32[16,1408]{0,1:T(8,128)S(1)} %copy.27), kind=kLoop, calls=%fused_computation.2 | loop fusion | flops 11534336 | bytes 34693120 | tf_op jit(solution)/shard_map/convert_element_type | solution.py:21
  147.7 89.5 %all-to-all-done = bf16[16,256,1408]{1,0,2:T(8,128)(2,1)} async-done(((bf16[16,256,1408]{1,0,2:T(8,128)(2,1)}), bf16[16,256,1408]{1,0,2:T(8,128)(2,1)}, u32[]{:S(2)}, u32[]{:S(2)}) %all-to-all-start) | async-done | bytes 11534368 | tf_op jit(solution)/shard_map/all_to_all | solution.py:25
  237.2 5.3 all-to-all-start.1
  242.5 9.8 %divide_convert_fusion = bf16[16,1408,256]{2,1,0:T(8,128)(2,1)S(1)} fusion(f32[16,1408,256]{2,1,0:T(8,128)} %param.7, f32[16,1408]{1,0:T(8,128)S(1)} %sqrt.11), kind=kLoop, calls=%fused_computation | loop fusion | flops 11534336 | bytes 34693120 | tf_op jit(solution)/shard_map/convert_element_type | solution.py:22
  252.3 1.2 fusion.7
  253.5 1.2 fusion.6
  254.7 1.2 fusion.5
  255.9 1.2 fusion.4
  257.1 1.2 fusion.3
  258.3 1.2 fusion.2
  259.5 1.2 fusion.1
  260.7 1.2 fusion
  261.9 108.3 %all-to-all-done.1 = bf16[16,256,1408]{1,0,2:T(8,128)(2,1)} async-done(((bf16[16,256,1408]{1,0,2:T(8,128)(2,1)}), bf16[16,256,1408]{1,0,2:T(8,128)(2,1)}, u32[]{:S(2)}, u32[]{:S(2)}) %all-to-all-start.1) | async-done | bytes 11534368 | tf_op jit(solution)/shard_map/all_to_all | solution.py:26
  370.2 5.3 all-to-all-start.2
  375.5 130.9 %all_gather.6 = bf16[2048,16]{0,1:T(8,128)(2,1)S(1)} all-gather(bf16[256,16]{0,1:T(8,128)(2,1)S(1)} %multiply_convert_fusion), channel_id=1, replica_groups=mesh['ep'=4,'fsdp'=8] {'fsdp'}, dimensions={0}, use_global_device_ids=true | all-gather | bytes 73728 | tf_op jit(solution)/shard_map/all_gather | solution.py:44
  506.4 14.0 %all_gather.7 = bf16[2048,64]{0,1:T(8,128)(2,1)S(1)} all-gather(bf16[2048,16]{0,1:T(8,128)(2,1)S(1)} %all_gather.6), channel_id=1, replica_groups=mesh['ep'=4,'fsdp'=8] {'ep'}, dimensions={1}, use_global_device_ids=true | all-gather | bytes 327680 | tf_op jit(solution)/shard_map/all_gather | solution.py:45
  520.4 0.7 constant_dynamic-slice_fusion.2
  522.4 11.3 %copy.26 = bf16[16,8,256,176]{2,1,3,0:T(8,128)(2,1)} copy(bf16[16,8,256,176]{2,0,3,1:T(8,128)(2,1)} %bitcast.2) | data formatting | bytes 23068672 | tf_op jit(solution)/shard_map/all_to_all | solution.py:25
  533.8 18.0 %all_to_all.32 = bf16[16,2048,176]{1,2,0:T(8,128)(2,1)} reshape(bf16[16,8,256,176]{2,1,3,0:T(8,128)(2,1)} %copy.26) | data formatting | bytes 23068672 | tf_op jit(solution)/shard_map/all_to_all | solution.py:25
  551.7 11.3 %copy.30 = bf16[16,8,256,176]{2,1,3,0:T(8,128)(2,1)} copy(bf16[16,8,256,176]{2,0,3,1:T(8,128)(2,1)} %bitcast.5) | data formatting | bytes 23068672 | tf_op jit(solution)/shard_map/all_to_all | solution.py:26
  563.1 18.0 %all_to_all.36 = bf16[16,2048,176]{1,2,0:T(8,128)(2,1)} reshape(bf16[16,8,256,176]{2,1,3,0:T(8,128)(2,1)} %copy.30) | data formatting | bytes 23068672 | tf_op jit(solution)/shard_map/all_to_all | solution.py:26
  581.0 10.0 %copy.34 = bf16[8,16,22,8,256]{4,3,0,2,1:T(8,128)(2,1)} copy(bf16[8,16,22,8,256]{4,3,2,1,0:T(8,128)(2,1)} %bitcast.15) | data formatting | bytes 23068672 | tf_op jit(solution)/shard_map/reshape | solution.py:28
  591.0 0.7 copy.46
  (19 shorter events, 2.0 us)
Async XLA Ops:
  7.2 81.6 %all-reduce.3.cloned.1.call-start = ((), (), s32[]{:S(2)}) async-start(), calls=%async_computation.3 | async-start | bytes 540672 | tf_op jit(solution)/shard_map/psum | solution.py:8
  7.2 14.2 %copy-start = (f32[16,256,1408]{2,1,0:T(8,128)S(1)}, f32[16,256,1408]{2,1,0:T(8,128)}, u32[]{:S(2)}) copy-start(f32[16,256,1408]{2,1,0:T(8,128)} %param.5) | copy-start | bytes 69206016
  104.2 133.0 %all-to-all-start = ((bf16[16,256,1408]{1,0,2:T(8,128)(2,1)}), bf16[16,256,1408]{1,0,2:T(8,128)(2,1)}, u32[]{:S(2)}, u32[]{:S(2)}) async-start(bf16[16,256,1408]{1,0,2:T(8,128)(2,1)} %divide_convert_fusion.2), calls=%async_computation | async-start | bytes 23068672 | tf_op jit(solution)/shard_map/all_to_all | solution.py:25
  109.4 23.7 %copy-start.2 = (f32[16,1408]{1,0:T(8,128)S(1)}, f32[16,1408]{1,0:T(8,128)}, u32[]{:S(2)}) copy-start(f32[16,1408]{1,0:T(8,128)} %get-tuple-element.8) | copy-start | bytes 270340
  147.7 94.8 %copy-start.1 = (f32[16,1408]{1,0:T(8,128)S(1)}, f32[16,1408]{1,0:T(8,128)}, u32[]{:S(2)}) copy-start(f32[16,1408]{1,0:T(8,128)} %get-tuple-element.9) | copy-start | bytes 270340
  237.2 133.0 %all-to-all-start.1 = ((bf16[16,256,1408]{1,0,2:T(8,128)(2,1)}), bf16[16,256,1408]{1,0,2:T(8,128)(2,1)}, u32[]{:S(2)}, u32[]{:S(2)}) async-start(bf16[16,256,1408]{1,0,2:T(8,128)(2,1)} %divide_convert_fusion.1), calls=%async_computation.1 | async-start | bytes 23068672 | tf_op jit(solution)/shard_map/all_to_all | solution.py:26
  261.9 113.6 %copy-start.3 = (f32[256,16]{0,1:T(8,128)S(1)}, f32[256,16]{0,1:T(8,128)}, u32[]{:S(2)}) copy-start(f32[256,16]{0,1:T(8,128)} %param.8) | copy-start | bytes 49156
  261.9 113.6 %copy-start.4 = (f32[256]{0:T(256)S(1)}, f32[256]{0:T(256)}, u32[]{:S(2)}) copy-start(f32[256]{0:T(256)} %param.9) | copy-start | bytes 3076
  370.2 210.8 %all-to-all-start.2 = ((bf16[8,16,176,256]{3,2,1,0:T(8,128)(2,1)}), bf16[8,16,176,256]{3,2,1,0:T(8,128)(2,1)}, u32[]{:S(2)}, u32[]{:S(2)}) async-start(bf16[8,16,176,256]{3,2,1,0:T(8,128)(2,1)} %fusion), calls=%async_computation.2 | async-start | bytes 23068672 | tf_op jit(solution)/shard_map/all_to_all | solution.py:29
Sparse Core Ops, SparseCore 0:
  32.6 56.1 all-reduce.2
